TPU v7x, 32 devices: a whole 2x2x4 slice. The times are simulated.
32 devices in a mesh: robot: 8 (over z, x), sub: 4 (over y, core).
Axes of the slice: x: 2, y: 2, z: 4, core: 2. Of those that a mesh axis runs over, the one named last changes fastest.
Arguments:
- landmark_copies: float32 [8, 4, 3, 512], P('robot', 'sub'), may hold values from -6 to 6
- dual_copies: float32 [8, 4, 3, 512], P('robot', 'sub'), may hold values from -4 to 4
- visibility: int32 [8, 4, 512], P('robot', 'sub'), may hold values from 0 to 511
- block_counts: int32 [8, 4, 8], P('robot', 'sub'), may hold values from 1 to 64, as said below
- consensus_old: float32 [8, 4, 3, 512], P('robot', 'sub'), may hold values from -6 to 6
- poses: float32 [8, 4, 6, 1024], P('robot', 'sub'), may hold values from -6 to 6
- inverse_blocks: float32 [8, 4, 36, 1024], P('robot', 'sub'), may hold values from -1.8 to 1.8
- jacobians: float32 [8, 4, 18, 4096], P('robot', 'sub'), may hold values from -3 to 3
- measurements: float32 [8, 4, 3, 4096], P('robot', 'sub'), may hold values from -6 to 6
- obs_pose: int32 [8, 4, 4096], P('robot', 'sub'), may hold values from 0 to 1023
- obs_slot: int32 [8, 4, 4096], P('robot', 'sub'), may hold values from 0 to 511, as said below
- edge_to: int32 [8, 4, 1024], P('robot', 'sub'), may hold values from 0 to 4095
- edge_offset: float32 [8, 4, 6, 1024], P('robot', 'sub'), may hold values from -3 to 3
Outputs:
- refined_poses: float32 [8, 4, 6, 1024], P('robot', 'sub')
- consensus: float32 [8, 4, 3, 512], P('robot', 'sub')
- dual_new: float32 [8, 4, 3, 512], P('robot', 'sub')
- residual_norms: float32 [2], replicated
Inputs may be any that keep to these rules, and one draw needn't show every extreme that they name: block_counts[r,s,d] counts the live slots at the head of block d; for every sub index some robot receives full blocks from every robot, which robot varies with the draw. `obs_slot`: each observation names a live slot of its own device.
All inputs are finite; a program needn't handle non-finite values.
Results may differ from a plain program's by a relative error of at most 0.0001.
Values sent between devices are 32-bit elements; how exact they have to be, the bound alone decides.
A program may use at most 64 MiB of HBM per device.

v0:
```python
import jax
import jax.numpy as jnp
from jax import lax
from jax.sharding import PartitionSpec as P

penalty = 2.0


def body(
    landmark_copies,
    dual_copies,
    visibility,
    block_counts,
    consensus_old,
    poses,
    inverse_blocks,
    jacobians,
    measurements,
    obs_pose,
    obs_slot,
    edge_to,
    edge_offset,
):
    copies = landmark_copies[0, 0]
    duals = dual_copies[0, 0]
    slot_ids = visibility[0]
    counts = block_counts[0, 0]
    old_estimate = consensus_old[0, 0]
    robots = lax.axis_size("robot")
    slot_count = copies.shape[1]
    block_size = slot_count // robots
    owned = old_estimate.shape[1]
    live_mask = (
        (jnp.arange(block_size)[None, :] < counts[:, None]).reshape(slot_count).astype(jnp.float32)
    )
    outgoing = jnp.concatenate([(copies + duals) * live_mask[None, :], live_mask[None, :]], axis=0)
    received, received_ids = (
        lax.all_to_all(outgoing, "robot", split_axis=1, concat_axis=1, tiled=True),
        lax.all_to_all(slot_ids, "robot", split_axis=1, concat_axis=1, tiled=True),
    )
    owner_ids = received_ids[0]
    totals = jax.vmap(lambda entries: jax.ops.segment_sum(entries, owner_ids, num_segments=owned))(
        received
    )
    consensus = (old_estimate + totals[:3]) / (1.0 + totals[3:4])
    returning = consensus[:, owner_ids]
    back = lax.all_to_all(returning, "robot", split_axis=1, concat_axis=1, tiled=True)
    differ = (copies - back) * live_mask[None, :]
    dual_new = duals + differ
    primal = jnp.sum(differ * differ)
    change = consensus - old_estimate
    dualsum = penalty * penalty * jnp.sum(totals[3:4] * change * change)
    primal_all, dual_all = lax.psum((primal, dualsum), ("robot", "sub"))
    landmark_total = owned * robots * lax.axis_size("sub")
    residual_norms = jnp.sqrt(jnp.stack([primal_all, dual_all]) / landmark_total)
    pose_block = poses[0, 0]
    pose_count = pose_block.shape[1]
    robot_all = lax.all_gather(pose_block, "sub", axis=1, tiled=True)
    pose_far = robot_all[:, edge_to[0, 0]]
    copies_at = copies[:, obs_slot[0, 0]]
    error = measurements[0, 0] - copies_at
    jac_rows = jacobians[0, 0].reshape(3, 6, error.shape[1])
    pull = jnp.sum(jac_rows * error[:, None, :], axis=0)
    pose_ids = obs_pose[0, 0]
    grad_obs = jax.vmap(
        lambda entries: jax.ops.segment_sum(entries, pose_ids, num_segments=pose_count)
    )(pull)
    grad = grad_obs + pose_far - pose_block - edge_offset[0, 0]
    inverse = inverse_blocks[0, 0].reshape(6, 6, pose_count)
    delta = jnp.sum(inverse * grad[None, :, :], axis=1)
    refined = pose_block + delta
    return (refined[None, None], consensus[None, None], dual_new[None, None], residual_norms)


def solution(mesh):
    return jax.shard_map(
        body,
        mesh=mesh,
        in_specs=(
            P("robot", "sub", None, None),
            P("robot", "sub", None, None),
            P("robot", "sub", None),
            P("robot", "sub", None),
            P("robot", "sub", None, None),
            P("robot", "sub", None, None),
            P("robot", "sub", None, None),
            P("robot", "sub", None, None),
            P("robot", "sub", None, None),
            P("robot", "sub", None),
            P("robot", "sub", None),
            P("robot", "sub", None),
            P("robot", "sub", None, None),
        ),
        out_specs=(
            P("robot", "sub", None, None),
            P("robot", "sub", None, None),
            P("robot", "sub", None, None),
            P(),
        ),
        check_vma=False,
    )
```

profile of v0, /device:TPU:0, one launch (start us, length us, event | category | flops | bytes accessed | tf_op | source)
XLA Modules:
  0.0 154.9 jit_solution(5562532823633209940)
XLA Ops:
  1.1 1.3 reduce.16
  3.2 7.3 %all-to-all-start = ((s32[1,8,64]{2,0,1:T(1,128)}), s32[1,8,64]{2,0,1:T(1,128)S(1)}, u32[]{:S(2)}, u32[]{:S(2)}) async-start(s32[1,8,64]{2,0,1:T(1,128)} %all_to_all.22), calls=%async_computation | async-start | bytes 8192 | tf_op jit(solution)/shard_map/all_to_all | solution.py:39
  11.9 0.8 copy.53
  12.7 0.7 add_reduce_fusion.1
  13.6 0.7 compare_select_fusion
  14.3 1.4 copy.52
  15.7 14.1 %gather_fusion.1 = f32[4096,3]{1,0:T(8,128)} fusion(f32[3,512]{0,1:T(8,128)S(1)} %bitcast.54, s32[4096]{0:T(1024)S(1)} %broadcast_clamp_fusion), kind=kCustom, calls=%fused_computation.1 | custom fusion | bytes 114688 | tf_op jit(solution)/shard_map/gather | solution.py:60
  29.8 3.2 %bitcast_subtract_fusion = f32[3,4096]{0,1:T(8,128)} fusion(f32[4096,3]{1,0:T(8,128)} %gather_fusion.1, f32[1,1,3,4096]{2,3,1,0:T(8,128)S(1)} %copy.52), kind=kLoop, calls=%fused_computation.5 | loop fusion | flops 12288 | bytes 147456 | tf_op jit(solution)/shard_map/sub | solution.py:61
  33.0 2.3 %copy.54 = f32[3,4096]{1,0:T(4,128)S(1)} copy(f32[3,4096]{0,1:T(8,128)} %bitcast_subtract_fusion) | data formatting | bytes 98304 | tf_op jit(solution)/shard_map/sub | solution.py:61
  36.1 2.0 %copy.55 = f32[4096,6]{1,0:T(8,128)} copy(f32[4096,6]{0,1:T(8,128)S(1)} %bitcast.57) | data formatting | bytes 196608 | tf_op jit(solution)/shard_map/reduce_sum | solution.py:63
  38.3 15.8 %all-gather = f32[1,1,6,4096]{2,3,1,0:T(8,128)S(1)} all-gather(f32[1,1,6,1024]{2,3,1,0:T(8,128)S(1)} %copy.51), channel_id=2, replica_groups=mesh['robot'=8,'sub'=4] {'sub'}, dimensions={3}, use_global_device_ids=true | all-gather | bytes 122880 | tf_op jit(solution)/shard_map/all_gather | solution.py:58
  54.1 1.0 copy.57
  55.1 2.8 %gather_fusion = f32[1024,6]{1,0:T(8,128)S(1)} fusion(f32[6,4096]{0,1:T(8,128)S(1)} %bitcast.55, s32[1024]{0:T(1024)S(1)} %broadcast_clamp_fusion.1), kind=kCustom, calls=%fused_computation | custom fusion | bytes 53248 | tf_op jit(solution)/shard_map/gather | solution.py:59
  58.0 22.9 %scatter_fusion = f32[6,1024]{0,1:T(8,128)S(1)} fusion(f32[6,1024]{0,1:T(8,128)S(1)} %bitcast.53, s32[4096]{0:T(1024)S(1)} %bitcast.67, f32[4096,6]{1,0:T(8,128)} %copy.55), kind=kCustom, calls=%fused_computation.3 | custom fusion | flops 24576 | bytes 311296 | tf_op jit(solution)/shard_map/vmap()/scatter-add | solution.py:66
  82.6 6.0 %all-to-all-start.1 = ((f32[8,1,256]{2,1,0:T(1,128)}), f32[8,1,256]{2,1,0:T(1,128)S(1)}, u32[]{:S(2)}, u32[]{:S(2)}) async-start(f32[8,1,256]{2,1,0:T(1,128)} %reshape.262), calls=%async_computation.1 | async-start | bytes 16384 | tf_op jit(solution)/shard_map/all_to_all | solution.py:38
  89.4 5.7 %all-to-all-done.1 = f32[8,1,256]{2,1,0:T(1,128)S(1)} async-done(((f32[8,1,256]{2,1,0:T(1,128)}), f32[8,1,256]{2,1,0:T(1,128)S(1)}, u32[]{:S(2)}, u32[]{:S(2)}) %all-to-all-start.1) | async-done | bytes 8224 | tf_op jit(solution)/shard_map/all_to_all | solution.py:38
  96.6 2.3 %scatter_custom_fusion.1 = f32[4,512]{0,1:T(8,128)S(1)} fusion(s32[512]{0:T(512)S(1)} %reshape.227, f32[512,4]{1,0:T(8,128)S(1)} %copy.62, f32[]{:T(128)} %constant.10.clone.1), kind=kCustom, calls=%fused_computation.21 | custom fusion | flops 2048 | bytes 8196 | tf_op jit(solution)/shard_map/vmap()/scatter-add | solution.py:42
  99.2 0.8 fusion
  100.0 1.0 gather_fusion.2
  101.9 3.3 %all-to-all-start.2 = ((f32[8,1,192]{2,1,0:T(1,128)}), f32[8,1,192]{2,1,0:T(1,128)S(1)}, u32[]{:S(2)}, u32[]{:S(2)}) async-start(f32[8,1,192]{2,1,0:T(1,128)} %reshape.264), calls=%async_computation.2 | async-start | bytes 16384 | tf_op jit(solution)/shard_map/all_to_all | solution.py:47
  107.3 4.4 %all-to-all-done.2 = f32[8,1,192]{2,1,0:T(1,128)S(1)} async-done(((f32[8,1,192]{2,1,0:T(1,128)}), f32[8,1,192]{2,1,0:T(1,128)S(1)}, u32[]{:S(2)}, u32[]{:S(2)}) %all-to-all-start.2) | async-done | bytes 6176 | tf_op jit(solution)/shard_map/all_to_all | solution.py:47
  112.7 0.7 fusion.4
  114.1 38.9 %all-reduce = (f32[1]{0:T(128)}, f32[1]{0:T(128)}) all-reduce(f32[1]{0:T(128)} %bitcast.22, f32[1]{0:T(128)} %bitcast.21), channel_id=1, replica_groups=mesh['robot'=8,'sub'=4] {'robot','sub'}, use_global_device_ids=true, to_apply=%region_7.0 | all-reduce | flops 2 | bytes 16 | tf_op jit(solution)/shard_map/psum | solution.py:53
  153.0 1.9 %fusion.10 = f32[2]{0:T(128)} fusion(f32[1]{0:T(128)} %get-tuple-element.22, f32[1]{0:T(128)} %get-tuple-element.23), kind=kLoop, calls=%fused_computation.41 | loop fusion | flops 4 | bytes 16 | tf_op jit(solution)/shard_map/sqrt | solution.py:55
  (67 shorter events, 11.8 us)
Async XLA Ops:
  3.2 79.4 %all-to-all-start = ((s32[1,8,64]{2,0,1:T(1,128)}), s32[1,8,64]{2,0,1:T(1,128)S(1)}, u32[]{:S(2)}, u32[]{:S(2)}) async-start(s32[1,8,64]{2,0,1:T(1,128)} %all_to_all.22), calls=%async_computation | async-start | bytes 8192 | tf_op jit(solution)/shard_map/all_to_all | solution.py:39
  33.0 2.3 %copy-start.1 = (f32[1,1,18,4096]{3,1,2,0:T(1,128)S(1)}, f32[1,1,18,4096]{3,1,2,0:T(1,128)}, u32[]{:S(2)}) copy-start(f32[1,1,18,4096]{3,1,2,0:T(1,128)} %param.20) | copy-start | bytes 884740
  35.2 2.8 %copy-start.3 = (f32[1,1,6,1024]{3,1,2,0:T(1,128)S(1)}, f32[1,1,6,1024]{3,1,2,0:T(1,128)}, u32[]{:S(2)}) copy-start(f32[1,1,6,1024]{3,1,2,0:T(1,128)} %param.18) | copy-start | bytes 73732
  38.1 16.0 %copy-start.9 = (s32[1,1,1024]{2,1,0:T(1,128)S(1)}, s32[1,1,1024]{2,1,0:T(1,128)}, u32[]{:S(2)}) copy-start(s32[1,1,1024]{2,1,0:T(1,128)} %param.24) | copy-start | bytes 12292
  38.1 16.0 %copy-start.5 = (f32[1,1,6,1024]{3,1,2,0:T(1,128)S(1)}, f32[1,1,6,1024]{3,1,2,0:T(1,128)}, u32[]{:S(2)}) copy-start(f32[1,1,6,1024]{3,1,2,0:T(1,128)} %param.25) | copy-start | bytes 73732
  38.1 19.9 %copy-start.7 = (s32[1,1,4096]{2,1,0:T(1,128)S(1)}, s32[1,1,4096]{2,1,0:T(1,128)}, u32[]{:S(2)}) copy-start(s32[1,1,4096]{2,1,0:T(1,128)} %param.22) | copy-start | bytes 49156
  57.9 23.0 %copy-start = (f32[1,1,6,1024]{2,3,1,0:T(8,128)S(1)}, f32[1,1,6,1024]{2,3,1,0:T(8,128)}, u32[]{:S(2)}) copy-start(f32[1,1,6,1024]{2,3,1,0:T(8,128)} %copy.57) | copy-start | bytes 73732
  58.0 23.2 %copy-start.2 = (f32[1,1,36,1024]{3,1,2,0:T(1,128)S(1)}, f32[1,1,36,1024]{3,1,2,0:T(1,128)}, u32[]{:S(2)}) copy-start(f32[1,1,36,1024]{3,1,2,0:T(1,128)} %param.19) | copy-start | bytes 442372
  80.9 1.5 copy-start.8
  81.6 31.9 %copy-start.4 = (f32[1,1,3,512]{3,1,2,0:T(1,128)S(1)}, f32[1,1,3,512]{3,1,2,0:T(1,128)}, u32[]{:S(2)}) copy-start(f32[1,1,3,512]{3,1,2,0:T(1,128)} %param.13) | copy-start | bytes 18436
  81.6 31.9 %copy-start.6 = (f32[1,1,3,512]{3,1,2,0:T(1,128)S(1)}, f32[1,1,3,512]{3,1,2,0:T(1,128)}, u32[]{:S(2)}) copy-start(f32[1,1,3,512]{3,1,2,0:T(1,128)} %param.14) | copy-start | bytes 18436
  82.6 12.5 %all-to-all-start.1 = ((f32[8,1,256]{2,1,0:T(1,128)}), f32[8,1,256]{2,1,0:T(1,128)S(1)}, u32[]{:S(2)}, u32[]{:S(2)}) async-start(f32[8,1,256]{2,1,0:T(1,128)} %reshape.262), calls=%async_computation.1 | async-start | bytes 16384 | tf_op jit(solution)/shard_map/all_to_all | solution.py:38
  101.9 9.8 %all-to-all-start.2 = ((f32[8,1,192]{2,1,0:T(1,128)}), f32[8,1,192]{2,1,0:T(1,128)S(1)}, u32[]{:S(2)}, u32[]{:S(2)}) async-start(f32[8,1,192]{2,1,0:T(1,128)} %reshape.264), calls=%async_computation.2 | async-start | bytes 16384 | tf_op jit(solution)/shard_map/all_to_all | solution.py:47
where the time goes:
time: 156 us; the launch traced here: 155 us
  blocking collectives  54.7 us (35%)
  other arithmetic  40.4 us (26%)
  local copies, waits for them, and re-layouts  31.6 us (20%)
  starting transfers between devices  16.6 us (11%)
  waiting for transfers between devices  10.1 us (6%)
  between operations  1.6 us (1%)
    psum x1, blocking collectives, body(): primal_all, dual_all = lax.psum((primal, dualsum), ('robot', 'sub'))  38.9 us
    scatter-add x1, other arithmetic, body(): jax.ops.segment_sum(entries, pose_ids, num_segments=pose_count)  22.9 us
    all_gather x1, blocking collectives, body(): robot_all = lax.all_gather(pose_block, 'sub', axis=1, tiled=True)  15.8 us
    gather x1, local copies, waits for them, and re-layouts, body(): copies_at = copies[:, obs_slot[0, 0]]  14.1 us
    all_to_all x1, starting transfers between devices, body(): lax.all_to_all(slot_ids, 'robot', split_axis=1, concat_axis=1, tiled=True)  7.28 us
    unnamed x32, local copies, waits for them, and re-layouts  7.06 us
    all_to_all x1, starting transfers between devices, body(): lax.all_to_all(outgoing, 'robot', split_axis=1, concat_axis=1, tiled=True)  6.01 us
    all_to_all x1, waiting for transfers between devices, body(): lax.all_to_all(outgoing, 'robot', split_axis=1, concat_axis=1, tiled=True)  5.69 us
  transfers between devices with their start and end apart: 3, of which 2 were waited for; matrix products, arithmetic and copies ran while one was open for 38% of the time, Pallas kernels for 0%

commit v1 on v0

v1 whole, which is shorter than its diff:
```python
import functools

import jax
import jax.numpy as jnp
from jax import lax
from jax.experimental import pallas as pl
from jax.experimental.pallas import tpu as pltpu
from jax.sharding import PartitionSpec as P

penalty = 2.0
LANES = 128
CHUNK = 8
MESH = pl.DeviceIdType.MESH
f32, bf16, i32 = jnp.float32, jnp.bfloat16, jnp.int32


def pieces(x):
    hi = x.astype(bf16).astype(f32)
    return hi, x - hi


def pad_rows(x, rows):
    return jnp.concatenate([x, jnp.zeros((rows - x.shape[0], x.shape[1]), x.dtype)], axis=0)


def strip(ref, first, count, tiles, start, length, at=()):
    parts = [
        ref[(*at, pl.ds(first * tiles + t, count, stride=tiles), slice(None))] if count > 1
        else ref[(*at, slice(first * tiles + t, first * tiles + t + 1), slice(None))]
        for t in range(start, start + length)
    ]
    return parts[0] if length == 1 else jnp.concatenate(parts, axis=1)


def stack_rows(ref, t):
    return jnp.concatenate([ref[k, t : t + 1, :] for k in range(ref.shape[0])], axis=0)


def one_hot(lo):
    rows = lax.broadcasted_iota(i32, (LANES, lo.shape[1]), 0)
    return jnp.where(rows == lo, 1.0, 0.0).astype(bf16)


def table(x, width):
    groups = []
    for h in range(x.shape[1] // width):
        hi, lo = pieces(pad_rows(x[:, h * width : (h + 1) * width], 8))
        groups.append(jnp.concatenate([hi, lo], axis=1))
    return jnp.concatenate(groups, axis=0).astype(bf16)


def pick(tab, hot, hi):
    found = jnp.dot(tab, jnp.concatenate([hot, hot], axis=0), preferred_element_type=f32)
    total = None
    for h in range(tab.shape[0] // 8):
        part = jnp.where(hi == h, found[h * 8 : h * 8 + 8], 0.0)
        total = part if total is None else total + part
    return total


def spread(values, hot, hi, tiles):
    a, b = pieces(values)
    both = jnp.concatenate([a, b], axis=0)
    lhs = jnp.concatenate([jnp.where(hi == h, both, 0.0) for h in range(tiles)], axis=0).astype(bf16)
    return lax.dot_general(lhs, hot, (((1,), (1,)), ((), ())), preferred_element_type=f32)


def kernel(
    robots, subs,
    copies_ref, duals_ref, vis_ref, counts_ref, old_ref, poses_ref, inv_ref, jac_ref, meas_ref,
    obs_pose_ref, obs_slot_ref, edge_to_ref, edge_off_ref,
    refined_ref, cons_ref, dual_ref, res_ref,
    outgoing, received, back_out, back_in, pose_in, part_out, part_in,
    send1, recv1, send2, recv2, sendp, recvp, send3, recv3,
):
    me_r = lax.axis_index("robot")
    me_s = lax.axis_index("sub")
    slot_tiles = vis_ref.shape[0]
    slots = slot_tiles * LANES
    block = slots // robots
    per = LANES // block
    tiles = old_ref.shape[1]
    owned = tiles * LANES
    pose_tiles = edge_to_ref.shape[0]
    obs_tiles = obs_slot_ref.shape[0]
    params = poses_ref.shape[0] // pose_tiles

    barrier = pltpu.get_barrier_semaphore()
    for k in range(1, robots):
        pl.semaphore_signal(barrier, inc=1, device_id={"robot": lax.rem(me_r + k, robots)}, device_id_type=MESH)
    for k in range(1, subs):
        pl.semaphore_signal(barrier, inc=1, device_id={"sub": lax.rem(me_s + k, subs)}, device_id_type=MESH)

    lane = lax.broadcasted_iota(i32, (1, LANES), 1)
    copies = jnp.concatenate([stack_rows(copies_ref, t) for t in range(slot_tiles)], axis=1)
    for t in range(slots // LANES):
        cut = slice(t * LANES, (t + 1) * LANES)
        base = jnp.concatenate(
            [
                copies[:, cut],
                stack_rows(duals_ref, t),
                jnp.zeros((1, LANES), f32),
                vis_ref[t : t + 1, :].astype(f32),
            ],
            axis=0,
        )
        row = lax.broadcasted_iota(i32, (8, LANES), 0)
        for j in range(per):
            d = t * per + j
            live = jnp.where(lane < counts_ref[0, 0, d], 1.0, 0.0)
            tile = base if j == 0 else pltpu.roll(base, LANES - j * block, 1)
            outgoing[d] = jnp.where(row == 6, live, tile)

    slot_tab = table(copies, LANES)

    def observe(c, acc):
        span = (obs_tiles, c * CHUNK, CHUNK)
        slot = strip(obs_slot_ref, 0, 1, *span)
        at = pick(slot_tab, one_hot(slot & (LANES - 1)), slot >> 7)
        error = strip(meas_ref, 0, 3, *span) - at[0:3]
        pull = None
        for k in range(3):
            term = strip(jac_ref, k * params, params, *span) * error[k : k + 1]
            pull = term if pull is None else pull + term
        pose = strip(obs_pose_ref, 0, 1, *span)
        out = spread(pad_rows(pull, 8), one_hot(pose & (LANES - 1)), pose >> 7, pose_tiles)
        return out if acc is None else acc + out

    pl.semaphore_wait(barrier, robots - 1 + subs - 1)

    first = []
    for k in range(1, robots):
        target = lax.rem(me_r + k, robots)
        copy = pltpu.make_async_remote_copy(
            src_ref=outgoing.at[target], dst_ref=received.at[k],
            send_sem=send1.at[k], recv_sem=recv1.at[k],
            device_id={"robot": target}, device_id_type=MESH,
        )
        copy.start()
        first.append(copy)
    pose_copies = []
    for k in range(1, subs):
        copy = pltpu.make_async_remote_copy(
            src_ref=poses_ref, dst_ref=pose_in.at[k],
            send_sem=sendp.at[k], recv_sem=recvp.at[k],
            device_id={"sub": lax.rem(me_s + k, subs)}, device_id_type=MESH,
        )
        copy.start()
        pose_copies.append(copy)

    chunks = obs_tiles // CHUNK
    half = chunks // 2
    acc = None
    for c in range(half):
        acc = observe(c, acc)

    for copy in first:
        copy.wait()

    group = 8
    totals = None
    entries = []
    for g in range(robots // group):
        blocks = [outgoing[me_r] if k == 0 else received[k] for k in range(g * group, (g + 1) * group)]
        entry = jnp.concatenate(blocks, axis=1)
        ids = entry[7:8].astype(i32)
        live = entry[6:7]
        hot = one_hot(ids & (LANES - 1))
        value = jnp.concatenate(
            [(entry[0:3] + entry[3:6]) * live, live, jnp.zeros((4, entry.shape[1]), f32)], axis=0
        )
        out = spread(value, hot, ids >> 7, tiles)
        totals = out if totals is None else totals + out
        entries.append((entry, hot, ids >> 7))
    new_tiles = []
    dual_part = jnp.zeros((1, LANES), f32)
    for h in range(tiles):
        total = totals[h * 16 : h * 16 + 8] + totals[h * 16 + 8 : h * 16 + 16]
        old = stack_rows(old_ref, h)
        seen = total[3:4]
        fresh = (old + total[0:3]) / (1.0 + seen)
        change = fresh - old
        dual_part += seen * jnp.sum(change * change, axis=0, keepdims=True)
        for a in range(3):
            cons_ref[a, h : h + 1, :] = fresh[a : a + 1]
        new_tiles.append(fresh)
    cons_tab = table(jnp.concatenate(new_tiles, axis=1), LANES)
    primal_part = jnp.zeros((1, LANES), f32)
    fresh_duals = []
    for entry, hot, hi in entries:
        back = pick(cons_tab, hot, hi)[0:3]
        differ = (entry[0:3] - back) * entry[6:7]
        squares = jnp.sum(differ * differ, axis=0, keepdims=True)
        for k in range(group):
            primal_part += squares[:, k * LANES : (k + 1) * LANES]
        fresh_duals.append(entry[3:6] + differ)
    tail = jnp.concatenate([primal_part, penalty * penalty * dual_part, jnp.zeros((3, LANES), f32)], axis=0)
    second = []
    for k in range(robots):
        g, j = divmod(k, group)
        tile = jnp.concatenate([fresh_duals[g][:, j * LANES : (j + 1) * LANES], tail], axis=0)
        if k == 0:
            back_in[me_r] = tile
        else:
            back_out[k] = tile
    for k in range(1, robots):
        copy = pltpu.make_async_remote_copy(
            src_ref=back_out.at[k], dst_ref=back_in.at[me_r],
            send_sem=send2.at[k], recv_sem=recv2.at[k],
            device_id={"robot": lax.rem(me_r + robots - k, robots)}, device_id_type=MESH,
        )
        copy.start()
        second.append(copy)

    for c in range(half, chunks):
        acc = observe(c, acc)

    for copy in second:
        copy.wait()
    part = back_in[0]
    for d in range(1, robots):
        part = part + back_in[d]
    part_out[...] = part
    third = []
    for k in range(1, subs):
        copy = pltpu.make_async_remote_copy(
            src_ref=part_out, dst_ref=part_in.at[k],
            send_sem=send3.at[k], recv_sem=recv3.at[k],
            device_id={"sub": lax.rem(me_s + k, subs)}, device_id_type=MESH,
        )
        copy.start()
        third.append(copy)

    for t in range(slots // LANES):
        tile = back_in[t * per]
        for j in range(1, per):
            moved = pltpu.roll(back_in[t * per + j], j * block, 1)
            tile = jnp.where(lane < j * block, tile, moved)
        for a in range(3):
            dual_ref[a, t : t + 1, :] = tile[a : a + 1]

    for copy in pose_copies:
        copy.wait()
    edge = strip(edge_to_ref, 0, 1, pose_tiles, 0, pose_tiles)
    hot = one_hot(edge & (LANES - 1))
    edge_hi = edge >> 7
    poses = strip(poses_ref, 0, params, pose_tiles, 0, pose_tiles)
    far = None
    for k in range(subs):
        owner = lax.rem(me_s + subs - k, subs)
        source = poses if k == 0 else strip(pose_in, 0, params, pose_tiles, 0, pose_tiles, (k,))
        part_far = pick(table(source, LANES), hot, edge_hi - owner * pose_tiles)
        far = part_far if far is None else far + part_far
    for t in range(pose_tiles):
        cut = slice(t * LANES, (t + 1) * LANES)
        here = poses[:, cut]
        grad = (acc[t * 16 : t * 16 + 8] + acc[t * 16 + 8 : t * 16 + 16] + far[:, cut])[0:params]
        grad = grad - here - strip(edge_off_ref, 0, params, pose_tiles, t, 1)
        for b in range(params):
            column = inv_ref[pl.ds(b * pose_tiles + t, params, stride=params * pose_tiles), :]
            here = here + column * grad[b : b + 1]
        refined_ref[pl.ds(t, params, stride=pose_tiles), :] = here

    for copy in third:
        copy.wait()
    for k in range(1, subs):
        part = part + part_in[k]
    sums = jnp.sum(part, axis=1, keepdims=True)
    norms = jnp.sqrt(sums / float(owned * robots * subs))
    res_ref[...] = jnp.where(lane == 0, norms[3:4], norms[4:5])


def body(*args):
    robots = lax.axis_size("robot")
    subs = lax.axis_size("sub")
    copies, consensus_old, poses = args[0], args[4], args[5]
    flat = [x if i == 3 else x.reshape(x.size // LANES, LANES) for i, x in enumerate(args)]
    for i in (0, 1, 4):
        flat[i] = args[i].reshape(args[i].shape[2], -1, LANES)
    vmem = pl.BlockSpec(memory_space=pltpu.VMEM)
    smem = pl.BlockSpec(memory_space=pltpu.SMEM)
    dma = pltpu.SemaphoreType.DMA
    refined, consensus, dual_new, norms = pl.pallas_call(
        functools.partial(kernel, robots, subs),
        out_shape=(
            jax.ShapeDtypeStruct(flat[5].shape, f32),
            jax.ShapeDtypeStruct(flat[4].shape, f32),
            jax.ShapeDtypeStruct(flat[0].shape, f32),
            jax.ShapeDtypeStruct((1, LANES), f32),
        ),
        in_specs=[smem if i == 3 else vmem for i in range(13)],
        out_specs=(vmem, vmem, vmem, vmem),
        scratch_shapes=[
            pltpu.VMEM((robots, 8, LANES), f32),
            pltpu.VMEM((robots, 8, LANES), f32),
            pltpu.VMEM((robots, 8, LANES), f32),
            pltpu.VMEM((robots, 8, LANES), f32),
            pltpu.VMEM((subs,) + flat[5].shape, f32),
            pltpu.VMEM((8, LANES), f32),
            pltpu.VMEM((subs, 8, LANES), f32),
            dma((robots,)), dma((robots,)), dma((robots,)), dma((robots,)),
            dma((subs,)), dma((subs,)), dma((subs,)), dma((subs,)),
        ],
        compiler_params=pltpu.CompilerParams(collective_id=0, has_side_effects=True),
    )(*flat)
    return (
        refined.reshape(poses.shape),
        consensus.reshape(consensus_old.shape),
        dual_new.reshape(copies.shape),
        norms[0, :2],
    )


def solution(mesh):
    four = P("robot", "sub", None, None)
    three = P("robot", "sub", None)
    return jax.shard_map(
        body,
        mesh=mesh,
        in_specs=(four, four, three, three, four, four, four, four, four, three, three, three, four),
        out_specs=(four, four, four, P()),
        check_vma=False,
    )
```

time: 156 us -> 24.9 us (0.16)
  blocking collectives: 54.7 us -> 0 us
  other arithmetic: 40.4 us -> 0 us
  local copies, waits for them, and re-layouts: 31.6 us -> 3.75 us
  Pallas kernels: 0 us -> 20.2 us
  starting transfers between devices: 16.6 us -> 0 us
  waiting for transfers between devices: 10.1 us -> 0 us
    psum x1 -> x0, blocking collectives: 38.9 us -> none  [body(): primal_all, dual_all = lax.psum((primal, dualsum), ('robot', 'sub'))]
    scatter-add x2 -> x0, other arithmetic: 25.2 us -> none  [the longest x1 22.9 us: body(): jax.ops.segment_sum(entries, pose_ids, num_segments=pose_count)]
    pallas_call x0 -> x1, Pallas kernels: none -> 20.2 us  [body(): pl.pallas_call(functools.partial(kernel, robots, subs), out_shape=(jax.Sh...]
    gather x3 -> x0, local copies, waits for them, and re-layouts: 17.9 us -> none  [the longest x1 14.1 us: body(): copies_at = copies[:, obs_slot[0, 0]]]
    all_to_all x3 -> x0, starting transfers between devices: 16.6 us -> none  [the longest x1 7.28 us: body(): lax.all_to_all(slot_ids, 'robot', split_axis=1, concat_axis=1, tiled=True)]
    all_gather x1 -> x0, blocking collectives: 15.8 us -> none  [body(): robot_all = lax.all_gather(pose_block, 'sub', axis=1, tiled=True)]
    all_to_all x3 -> x0, waiting for transfers between devices: 10.1 us -> none  [the longest x1 5.69 us: body(): lax.all_to_all(outgoing, 'robot', split_axis=1, concat_axis=1, tiled=True)]
    unnamed x32 -> x9, local copies, waits for them, and re-layouts: 7.06 us -> 3.24 us
  transfers between devices with their start and end apart: 3 -> 0, of which waited for: 2 -> 0; matrix products, arithmetic and copies ran while one was open for 38% -> 0% of each run, Pallas kernels for 0% -> 0%
where the time goes in v1:
time: 24.9 us; the launch traced here: 24.7 us
  Pallas kernels  20.2 us (81%)
  local copies, waits for them, and re-layouts  3.75 us (15%)
  between operations  0.66 us (3%)
    pallas_call x1, Pallas kernels, body(): pl.pallas_call(functools.partial(kernel, robots, subs), out_shape=(jax.Sh...  20.2 us
    unnamed x9, local copies, waits for them, and re-layouts  3.24 us
    squeeze x1, local copies, waits for them, and re-layouts, body(): norms[0, :2]  0.51 us

profile of v1, /device:TPU:0, one launch (start us, length us, event | category | flops | bytes accessed | tf_op | source)
XLA Modules:
  0.0 24.7 jit_solution(17902112353114983256)
XLA Ops:
  0.6 20.2 %shard_map.156 = (f32[48,128]{1,0:T(8,128)}, f32[3,4,128]{2,1,0:T(4,128)}, f32[3,4,128]{2,1,0:T(4,128)}, f32[1,128]{1,0:T(1,128)}) custom-call(f32[3,4,128]{2,1,0:T(4,128)} %bitcast.25, f32[3,4,128]{2,1,0:T(4,128)} %bitcast.26, s32[4,128]{1,0:T(4,128)} %bitcast.31, s32[1,1,8]{2,1,0:T(1,128)} %counts_ref.1, f32[3,4,128]{2,1,0:T(4,128)} %bitcast.27, ...), custom_call_target="tpu_custom_call" | custom-call | tf_op jit(solution)/shard_map/pallas_call | solution.py:283
  20.9 0.0 copy-start.2
  20.9 0.6 %copy-done.2 = f32[1,128]{1,0:T(1,128)S(1)} copy-done((f32[1,128]{1,0:T(1,128)S(1)}, f32[1,128]{1,0:T(1,128)}, u32[]{:S(2)}) %copy-start.2) | copy-done | bytes 536
  21.5 0.5 %slice_bitcast_fusion = f32[2]{0:T(128)} fusion(f32[1,128]{1,0:T(1,128)S(1)} %copy-done.2), kind=kLoop, calls=%fused_computation | loop fusion | bytes 16 | tf_op jit(solution)/shard_map/squeeze | solution.py:310
  22.0 0.0 copy-start.1
  22.0 1.4 %copy.26 = f32[1,1,6,1024]{3,1,2,0:T(1,128)} copy(f32[1,1,6,1024]{3,1,2,0:T(1,128)} %bitcast.22) | data formatting | bytes 49152
  23.4 0.0 copy-done.1
  23.4 0.0 copy-start
  23.4 0.6 %copy.27 = f32[1,1,3,512]{3,1,2,0:T(1,128)} copy(f32[1,1,3,512]{3,1,2,0:T(1,128)S(1)} %bitcast.29) | data formatting | bytes 12288
  24.0 0.1 copy-done
  24.1 0.6 %copy.28 = f32[1,1,3,512]{3,1,2,0:T(1,128)} copy(f32[1,1,3,512]{3,1,2,0:T(1,128)S(1)} %bitcast.28) | data formatting | bytes 12288
Async XLA Ops:
  20.9 0.6 %copy-start.2 = (f32[1,128]{1,0:T(1,128)S(1)}, f32[1,128]{1,0:T(1,128)}, u32[]{:S(2)}) copy-start(f32[1,128]{1,0:T(1,128)} %get-tuple-element.11) | copy-start | bytes 1540
  22.0 1.4 %copy-start.1 = (f32[3,4,128]{2,1,0:T(4,128)S(1)}, f32[3,4,128]{2,1,0:T(4,128)}, u32[]{:S(2)}) copy-start(f32[3,4,128]{2,1,0:T(4,128)} %get-tuple-element.9) | copy-start | bytes 18436
  23.4 0.7 %copy-start = (f32[3,4,128]{2,1,0:T(4,128)S(1)}, f32[3,4,128]{2,1,0:T(4,128)}, u32[]{:S(2)}) copy-start(f32[3,4,128]{2,1,0:T(4,128)} %get-tuple-element.10) | copy-start | bytes 18436

commit v2 on v1

v2 whole, which is shorter than its diff:
```python
import functools

import jax
import jax.numpy as jnp
from jax import lax
from jax.experimental import pallas as pl
from jax.experimental.pallas import tpu as pltpu
from jax.sharding import PartitionSpec as P

penalty = 2.0
LANES = 128
CHUNK = 8
MESH = pl.DeviceIdType.MESH
f32, bf16, i32 = jnp.float32, jnp.bfloat16, jnp.int32


def pieces(x):
    hi = x.astype(bf16).astype(f32)
    return hi, x - hi


def pad_rows(x, rows):
    return jnp.concatenate([x, jnp.zeros((rows - x.shape[0], x.shape[1]), x.dtype)], axis=0)


def strip(ref, first, count, tiles, start, length, at=()):
    parts = [
        ref[(*at, pl.ds(first * tiles + t, count, stride=tiles), slice(None))] if count > 1
        else ref[(*at, slice(first * tiles + t, first * tiles + t + 1), slice(None))]
        for t in range(start, start + length)
    ]
    return parts[0] if length == 1 else jnp.concatenate(parts, axis=1)


def stack_rows(ref, t):
    return jnp.concatenate([ref[k, t : t + 1, :] for k in range(ref.shape[0])], axis=0)


def one_hot(lo):
    rows = lax.broadcasted_iota(i32, (LANES, lo.shape[1]), 0)
    return jnp.where(rows == lo, 1.0, 0.0).astype(bf16)


def table(x, width):
    groups = []
    for h in range(x.shape[1] // width):
        hi, lo = pieces(pad_rows(x[:, h * width : (h + 1) * width], 8))
        groups.append(jnp.concatenate([hi, lo], axis=1))
    return jnp.concatenate(groups, axis=0).astype(bf16)


def pick(tab, hot, hi):
    found = jnp.dot(tab, jnp.concatenate([hot, hot], axis=0), preferred_element_type=f32)
    total = None
    for h in range(tab.shape[0] // 8):
        part = jnp.where(hi == h, found[h * 8 : h * 8 + 8], 0.0)
        total = part if total is None else total + part
    return total


def spread(values, hot, hi, tiles):
    a, b = pieces(values)
    both = jnp.concatenate([a, b], axis=0)
    lhs = jnp.concatenate([jnp.where(hi == h, both, 0.0) for h in range(tiles)], axis=0).astype(bf16)
    return lax.dot_general(lhs, hot, (((1,), (1,)), ((), ())), preferred_element_type=f32)


def kernel(robots, subs, *refs):
    sources, refs = refs[:13], refs[13:]
    (refined_ref, cons_ref, dual_ref, res_ref), refs = refs[:4], refs[4:]
    staged, refs = refs[:13], refs[13:]
    (
        copies_ref, duals_ref, vis_ref, counts_ref, old_ref, poses_ref, inv_ref, jac_ref, meas_ref,
        obs_pose_ref, obs_slot_ref, edge_to_ref, edge_off_ref,
    ) = staged
    (
        outgoing, received, back_out, back_in, pose_in, part_out, part_in,
        load_sem, send1, recv1, send2, recv2, sendp, recvp, send3, recv3,
    ) = refs
    me_r = lax.axis_index("robot")
    me_s = lax.axis_index("sub")
    slot_tiles = vis_ref.shape[0]
    slots = slot_tiles * LANES
    block = slots // robots
    per = LANES // block
    tiles = old_ref.shape[1]
    owned = tiles * LANES
    pose_tiles = edge_to_ref.shape[0]
    obs_tiles = obs_slot_ref.shape[0]
    params = poses_ref.shape[0] // pose_tiles
    robot_steps = sorted(range(1, robots), key=lambda k: -min(k, robots - k))

    barrier = pltpu.get_barrier_semaphore()
    peers = [(kr, ks) for kr in [*robot_steps, 0] for ks in range(subs) if (kr, ks) != (0, 0)]
    for kr, ks in peers:
        there = (lax.rem(me_r + kr, robots), lax.rem(me_s + ks, subs))
        pl.semaphore_signal(barrier, inc=1, device_id=there, device_id_type=MESH)

    loads = [pltpu.make_async_copy(sources[i], staged[i], load_sem.at[i]) for i in range(13)]
    order = (0, 1, 2, 3, 10, 8, 7, 9, 5, 4, 11, 12, 6)
    for i in order:
        loads[i].start()

    lane = lax.broadcasted_iota(i32, (1, LANES), 1)
    row = lax.broadcasted_iota(i32, (8, LANES), 0)
    my_part = lax.rem(me_r, per)
    for i in order[:4]:
        loads[i].wait()
    copies = jnp.concatenate([stack_rows(copies_ref, t) for t in range(slot_tiles)], axis=1)
    for t in range(slot_tiles):
        cut = slice(t * LANES, (t + 1) * LANES)
        base = jnp.concatenate(
            [copies[:, cut], stack_rows(duals_ref, t), jnp.zeros((1, LANES), f32), vis_ref[t : t + 1, :].astype(f32)],
            axis=0,
        )
        for j in range(per):
            d = t * per + j
            tile = base
            for p in range(per):
                if p != j:
                    moved = pltpu.roll(base, (p - j) * block % LANES, 1)
                    tile = jnp.where(my_part == p, moved, tile)
            live = jnp.where(lane - my_part * block < counts_ref[0, 0, d], 1.0, 0.0)
            outgoing[d] = jnp.where(row == 6, live, tile)

    slot_tab = table(copies, LANES)
    for i in order[4:]:
        loads[i].wait()

    def observe(c, acc):
        span = (obs_tiles, c * CHUNK, CHUNK)
        slot = strip(obs_slot_ref, 0, 1, *span)
        at = pick(slot_tab, one_hot(slot & (LANES - 1)), slot >> 7)
        error = strip(meas_ref, 0, 3, *span) - at[0:3]
        pull = None
        for k in range(3):
            term = strip(jac_ref, k * params, params, *span) * error[k : k + 1]
            pull = term if pull is None else pull + term
        pose = strip(obs_pose_ref, 0, 1, *span)
        out = spread(pad_rows(pull, 8), one_hot(pose & (LANES - 1)), pose >> 7, pose_tiles)
        return out if acc is None else acc + out

    acc = None
    for c in range(obs_tiles // CHUNK):
        acc = observe(c, acc)

    edge = strip(edge_to_ref, 0, 1, pose_tiles, 0, pose_tiles)
    edge_hot = one_hot(edge & (LANES - 1))
    edge_hi = edge >> 7
    poses = strip(poses_ref, 0, params, pose_tiles, 0, pose_tiles)
    far = pick(table(poses, LANES), edge_hot, edge_hi - me_s * pose_tiles)
    grads = []
    for t in range(pose_tiles):
        cut = slice(t * LANES, (t + 1) * LANES)
        grad = (acc[t * 16 : t * 16 + 8] + acc[t * 16 + 8 : t * 16 + 16] + far[:, cut])[0:params]
        grads.append(grad - poses[:, cut] - strip(edge_off_ref, 0, params, pose_tiles, t, 1))
    grad = jnp.concatenate(grads, axis=1)

    pl.semaphore_wait(barrier, len(peers))

    first = []
    for k in robot_steps:
        target = lax.rem(me_r + k, robots)
        copy = pltpu.make_async_remote_copy(
            src_ref=outgoing.at[target], dst_ref=received.at[k],
            send_sem=send1.at[k], recv_sem=recv1.at[k],
            device_id={"robot": target}, device_id_type=MESH,
        )
        copy.start()
        first.append(copy)
    pose_copies = []
    for k in range(1, subs):
        copy = pltpu.make_async_remote_copy(
            src_ref=poses_ref, dst_ref=pose_in.at[k],
            send_sem=sendp.at[k], recv_sem=recvp.at[k],
            device_id={"sub": lax.rem(me_s + k, subs)}, device_id_type=MESH,
        )
        copy.start()
        pose_copies.append(copy)

    for copy in first:
        copy.wait_recv()

    merged = []
    for g in range(robots // per):
        tile = None
        for j in range(per):
            k = g * per + j
            one = outgoing[me_r] if k == 0 else received[k]
            place = lax.rem(me_r + robots - k, per)
            mine = lane >= place * block
            tile = one if tile is None else jnp.where(mine & (lane < place * block + block), one, tile)
        merged.append(tile)
    group = min(8, len(merged))
    totals = None
    entries = []
    for g in range(0, len(merged), group):
        entry = jnp.concatenate(merged[g : g + group], axis=1)
        ids = entry[7:8].astype(i32)
        live = entry[6:7]
        hot = one_hot(ids & (LANES - 1))
        value = jnp.concatenate(
            [(entry[0:3] + entry[3:6]) * live, live, jnp.zeros((4, entry.shape[1]), f32)], axis=0
        )
        out = spread(value, hot, ids >> 7, tiles)
        totals = out if totals is None else totals + out
        entries.append((entry, hot, ids >> 7))
    new_tiles = []
    dual_part = jnp.zeros((1, LANES), f32)
    for h in range(tiles):
        total = totals[h * 16 : h * 16 + 8] + totals[h * 16 + 8 : h * 16 + 16]
        old = stack_rows(old_ref, h)
        seen = total[3:4]
        fresh = (old + total[0:3]) / (1.0 + seen)
        change = fresh - old
        dual_part += seen * jnp.sum(change * change, axis=0, keepdims=True)
        for a in range(3):
            cons_ref[a, h : h + 1, :] = fresh[a : a + 1]
        new_tiles.append(fresh)
    cons_tab = table(jnp.concatenate(new_tiles, axis=1), LANES)
    primal_part = jnp.zeros((1, LANES), f32)
    g = 0
    for entry, hot, hi in entries:
        back = pick(cons_tab, hot, hi)[0:3]
        differ = (entry[0:3] - back) * entry[6:7]
        squares = jnp.sum(differ * differ, axis=0, keepdims=True)
        fresh_dual = pad_rows(entry[3:6] + differ, 8)
        for k in range(entry.shape[1] // LANES):
            cut = slice(k * LANES, (k + 1) * LANES)
            primal_part += squares[:, cut]
            back_out[g] = fresh_dual[:, cut]
            g += 1
    part = jnp.concatenate([primal_part, penalty * penalty * dual_part], axis=0)
    part_out[...] = part
    back_in[me_r] = back_out[0]

    second = []
    for k in robot_steps:
        copy = pltpu.make_async_remote_copy(
            src_ref=back_out.at[k // per], dst_ref=back_in.at[me_r],
            send_sem=send2.at[k], recv_sem=recv2.at[k],
            device_id={"robot": lax.rem(me_r + robots - k, robots)}, device_id_type=MESH,
        )
        copy.start()
        second.append(copy)
    third = []
    for kr, ks in peers:
        n = kr * subs + ks
        copy = pltpu.make_async_remote_copy(
            src_ref=part_out, dst_ref=part_in.at[n],
            send_sem=send3.at[n], recv_sem=recv3.at[n],
            device_id=(lax.rem(me_r + kr, robots), lax.rem(me_s + ks, subs)), device_id_type=MESH,
        )
        copy.start()
        third.append(copy)

    for copy in pose_copies:
        copy.wait()
    for k in range(1, subs):
        owner = lax.rem(me_s + subs - k, subs)
        source = strip(pose_in, 0, params, pose_tiles, 0, pose_tiles, (k,))
        grad = grad + pick(table(source, LANES), edge_hot, edge_hi - owner * pose_tiles)[0:params]
    for t in range(pose_tiles):
        cut = slice(t * LANES, (t + 1) * LANES)
        here = poses[:, cut]
        for b in range(params):
            column = inv_ref[pl.ds(b * pose_tiles + t, params, stride=params * pose_tiles), :]
            here = here + column * grad[b : b + 1, cut]
        refined_ref[pl.ds(t, params, stride=pose_tiles), :] = here

    for copy in first:
        copy.wait_send()
    for copy in second:
        copy.wait()
    for t in range(slot_tiles):
        tile = None
        for j in range(per):
            raw = back_in[t * per + j]
            one = raw
            for p in range(per):
                if p != j:
                    moved = pltpu.roll(raw, (j - p) * block % LANES, 1)
                    one = jnp.where(my_part == p, moved, one)
            tile = one if tile is None else jnp.where(lane < j * block, tile, one)
        for a in range(3):
            dual_ref[a, t : t + 1, :] = tile[a : a + 1]

    for copy in third:
        copy.wait()
    for kr, ks in peers:
        part = part + part_in[kr * subs + ks]
    sums = jnp.sum(part, axis=1, keepdims=True)
    norms = jnp.sqrt(sums / float(owned * robots * subs))
    res_ref[...] = jnp.where(lane == 0, norms[0:1], norms[1:2])


def write_out(refined, consensus, dual_new, norms, refined_ref, cons_ref, dual_ref, res_ref):
    refined_ref[...] = refined[...]
    cons_ref[...] = consensus[...]
    dual_ref[...] = dual_new[...]
    res_ref[...] = norms[0, 0:2]


def body(*args):
    robots = lax.axis_size("robot")
    subs = lax.axis_size("sub")
    copies, consensus_old, poses = args[0], args[4], args[5]
    flat = [x if i == 3 else x.reshape(x.size // LANES, LANES) for i, x in enumerate(args)]
    for i in (0, 1, 4):
        flat[i] = args[i].reshape(args[i].shape[2], -1, LANES)
    vmem = pl.BlockSpec(memory_space=pltpu.VMEM)
    dma = pltpu.SemaphoreType.DMA
    everyone = robots * subs
    shapes = [flat[5].shape, flat[4].shape, flat[0].shape]
    held = pl.pallas_call(
        functools.partial(kernel, robots, subs),
        out_shape=tuple(pltpu.VMEM(shape, f32) for shape in [*shapes, (1, LANES)]),
        in_specs=[pl.BlockSpec(memory_space=pl.ANY)] * 13,
        out_specs=(vmem,) * 4,
        scratch_shapes=[
            *[(pltpu.SMEM if i == 3 else pltpu.VMEM)(x.shape, x.dtype) for i, x in enumerate(flat)],
            pltpu.VMEM((robots, 8, LANES), f32),
            pltpu.VMEM((robots, 8, LANES), f32),
            pltpu.VMEM((robots, 8, LANES), f32),
            pltpu.VMEM((robots, 8, LANES), f32),
            pltpu.VMEM((subs,) + flat[5].shape, f32),
            pltpu.VMEM((2, LANES), f32),
            pltpu.VMEM((everyone, 2, LANES), f32),
            dma((13,)),
            dma((robots,)), dma((robots,)), dma((robots,)), dma((robots,)),
            dma((subs,)), dma((subs,)), dma((everyone,)), dma((everyone,)),
        ],
        compiler_params=pltpu.CompilerParams(collective_id=0, has_side_effects=True),
    )(*flat)
    refined, consensus, dual_new, norms = pl.pallas_call(
        write_out,
        out_shape=tuple(jax.ShapeDtypeStruct(shape, f32) for shape in [*shapes, (2,)]),
        in_specs=[vmem] * 4,
        out_specs=(vmem,) * 4,
    )(*[pltpu.with_memory_space_constraint(x, pltpu.VMEM) for x in held])
    return (
        refined.reshape(poses.shape),
        consensus.reshape(consensus_old.shape),
        dual_new.reshape(copies.shape),
        norms,
    )


def solution(mesh):
    four = P("robot", "sub", None, None)
    three = P("robot", "sub", None)
    return jax.shard_map(
        body,
        mesh=mesh,
        in_specs=(four, four, three, three, four, four, four, four, four, three, three, three, four),
        out_specs=(four, four, four, P()),
        check_vma=False,
    )
```

time: 24.9 us -> 18.8 us (0.76)
  local copies, waits for them, and re-layouts: 3.75 us -> 0 us
  Pallas kernels: 20.2 us -> 17.9 us
    unnamed x9 -> x0, local copies, waits for them, and re-layouts: 3.24 us -> none
    pallas_call x1 -> x2, Pallas kernels: 20.2 us -> 17.9 us  [the longest x1 17.3 us: body(): pl.pallas_call(functools.partial(kernel, robots, subs), out_shape=tuple((...]
    squeeze x1 -> x0, local copies, waits for them, and re-layouts: 0.51 us -> none  [body(): norms[0, :2]]
where the time goes in v2:
time: 18.8 us; the launch traced here: 18.6 us
  Pallas kernels  17.9 us (95%)
  between operations  0.64 us (3%)
    pallas_call x1, Pallas kernels, body(): pl.pallas_call(functools.partial(kernel, robots, subs), out_shape=tuple((...  17.3 us
    pallas_call x1, Pallas kernels, body(): pl.pallas_call(write_out, out_shape=tuple((jax.ShapeDtypeStruct(shape, f3...  0.62 us

profile of v2, /device:TPU:0, one launch (start us, length us, event | category | flops | bytes accessed | tf_op | source)
XLA Modules:
  0.0 18.6 jit_solution(10177155277630447933)
XLA Ops:
  0.6 17.3 %shard_map.156 = (f32[48,128]{1,0:T(8,128)S(1)}, f32[3,4,128]{2,1,0:T(4,128)S(1)}, f32[3,4,128]{2,1,0:T(4,128)S(1)}, f32[1,128]{1,0:T(1,128)S(1)}) custom-call(f32[3,4,128]{2,1,0:T(4,128)} %bitcast.22, f32[3,4,128]{2,1,0:T(4,128)} %bitcast.23, s32[4,128]{1,0:T(4,128)} %bitcast.26, s32[1,1,8]{2,1,0:T(1,128)} %refs_3_.1, f32[3,4,128]{2,1,0:T(4,128)} %bitcast.24, ...), custom_call_target="tpu_custom_call" | custom-call | tf_op jit(solution)/shard_map/pallas_call | solution.py:315
  18.0 0.6 %shard_map.157 = (f32[48,128]{1,0:T(8,128)}, f32[3,4,128]{2,1,0:T(4,128)}, f32[3,4,128]{2,1,0:T(4,128)}, f32[2]{0:T(128)}) custom-call(f32[48,128]{1,0:T(8,128)S(1)} %get-tuple-element.12.refined, f32[3,4,128]{2,1,0:T(4,128)S(1)} %get-tuple-element.13.consensus, f32[3,4,128]{2,1,0:T(4,128)S(1)} %get-tuple-element.14.dual_new, ...), custom_call_target="tpu_custom_call" | custom-call | tf_op jit(solution)/shard_map/pallas_call | solution.py:335
